TPU v7x, 32 devices: a whole 2x2x4 slice. The times are simulated.
32 devices in a mesh: unit: 1, dp: 16 (over z, y, x), ens: 2 (over core).
Axes of the slice: x: 2, y: 2, z: 4, core: 2. Of those that a mesh axis runs over, the one named last changes fastest.
Arguments:
- samples_in: bfloat16 [4096, 4096], P(('unit', 'dp'), 'ens'), may hold values from -3 to 3, as said below
- second_samples_in: bfloat16 [4096, 4096], P(('unit', 'dp'), 'ens'), may hold values from -3 to 3, as said below
Outputs:
- scaled: float32 [4096, 4096], P('unit', ('ens', 'dp'))
- second_scaled: float32 [4096, 4096], P('unit', ('ens', 'dp'))
Inputs may be any that keep to these rules, and one draw needn't show every extreme that they name: samples_in holds numbers from -3 to 3. second_samples_in holds numbers from -3 to 3.
All inputs are finite; a program needn't handle non-finite values.
Results may differ from a plain program's by a relative error of at most 0.00035.
Values may be sent and summed in bfloat16 or wider, within the bound.
A program may use at most 128 MiB of HBM per device.

v0:
```python
import jax
import jax.numpy as jnp
from jax import lax
from jax.sharding import PartitionSpec as P


def per_device(samples_in, second_samples_in):
    moved_samples_in, moved_second_samples_in = (
        lax.all_to_all(samples_in, "dp", split_axis=1, concat_axis=0, tiled=True),
        lax.all_to_all(second_samples_in, "dp", split_axis=1, concat_axis=0, tiled=True),
    )
    wide_scaled = moved_samples_in.astype(jnp.float32)
    power_scaled = jnp.exp(wide_scaled)
    sum_scaled = jnp.sum(power_scaled, axis=0)
    scaled = power_scaled / sum_scaled * moved_samples_in.shape[0]
    wide_second_scaled = moved_second_samples_in.astype(jnp.float32)
    power_second_scaled = jnp.exp(wide_second_scaled)
    sum_second_scaled = jnp.sum(power_second_scaled, axis=0)
    second_scaled = power_second_scaled / sum_second_scaled * moved_second_samples_in.shape[0]
    return (scaled, second_scaled)


def solution(mesh):
    placed = (P(("unit", "dp"), "ens"), P(("unit", "dp"), "ens"))
    return jax.shard_map(
        per_device,
        mesh=mesh,
        in_specs=placed,
        out_specs=(P("unit", ("ens", "dp")), P("unit", ("ens", "dp"))),
        check_vma=False,
    )
```

profile of v0, /device:TPU:8, one launch (start us, length us, event | category | flops | bytes accessed | tf_op | source)
XLA Modules:
  0.0 66.8 jit_solution(8155692977923089948)
XLA Ops:
  0.6 0.0 copy-start
  0.6 1.2 %copy-done = bf16[256,2048]{1,0:T(8,128)(2,1)S(1)} copy-done((bf16[256,2048]{1,0:T(8,128)(2,1)S(1)}, bf16[256,2048]{1,0:T(8,128)(2,1)}, u32[]{:S(2)}) %copy-start) | copy-done | bytes 1048600
  1.9 0.0 copy-start.1
  1.9 1.2 %copy_bitcast_fusion = bf16[256,16,128]{2,0,1:T(8,128)(2,1)} fusion(bf16[256,2048]{1,0:T(8,128)(2,1)S(1)} %copy-done), kind=kLoop, calls=%fused_computation.6 | loop fusion | bytes 2097152 | tf_op jit(solution)/shard_map/all_to_all | solution.py:10
  3.1 7.2 %all-to-all-start.1 = ((bf16[256,16,128]{2,0,1:T(8,128)(2,1)}), bf16[256,16,128]{2,0,1:T(8,128)(2,1)S(1)}, u32[]{:S(2)}, u32[]{:S(2)}) async-start(bf16[256,16,128]{2,0,1:T(8,128)(2,1)} %copy_bitcast_fusion), calls=%async_computation.1 | async-start | bytes 2097152 | tf_op jit(solution)/shard_map/all_to_all | solution.py:10
  10.3 0.0 copy-done.1
  10.3 1.2 %copy_bitcast_fusion.1 = bf16[256,16,128]{2,0,1:T(8,128)(2,1)} fusion(bf16[256,2048]{1,0:T(8,128)(2,1)S(1)} %copy-done.1), kind=kLoop, calls=%fused_computation.7 | loop fusion | bytes 2097152 | tf_op jit(solution)/shard_map/all_to_all | solution.py:9
  11.6 24.3 %all-to-all-done.1 = bf16[256,16,128]{2,0,1:T(8,128)(2,1)S(1)} async-done(((bf16[256,16,128]{2,0,1:T(8,128)(2,1)}), bf16[256,16,128]{2,0,1:T(8,128)(2,1)S(1)}, u32[]{:S(2)}, u32[]{:S(2)}) %all-to-all-start.1) | async-done | bytes 1048608 | tf_op jit(solution)/shard_map/all_to_all | solution.py:10
  35.9 4.7 %all-to-all-start = ((bf16[256,16,128]{2,0,1:T(8,128)(2,1)}), bf16[256,16,128]{2,0,1:T(8,128)(2,1)S(1)}, u32[]{:S(2)}, u32[]{:S(2)}) async-start(bf16[256,16,128]{2,0,1:T(8,128)(2,1)} %copy_bitcast_fusion.1), calls=%async_computation | async-start | bytes 2097152 | tf_op jit(solution)/shard_map/all_to_all | solution.py:9
  40.6 0.6 fusion.3
  41.2 1.5 %fusion = f32[4096,128]{1,0:T(8,128)} fusion(f32[256,16,128]{2,0,1:T(8,128)S(1)} %get-tuple-element.3, f32[128]{0:T(128)S(1)} %get-tuple-element.2), kind=kLoop, calls=%fused_computation.1 | loop fusion | flops 1048576 | bytes 4194816 | tf_op jit(solution)/shard_map/mul | solution.py:19
  42.6 22.1 %all-to-all-done = bf16[256,16,128]{2,0,1:T(8,128)(2,1)S(1)} async-done(((bf16[256,16,128]{2,0,1:T(8,128)(2,1)}), bf16[256,16,128]{2,0,1:T(8,128)(2,1)S(1)}, u32[]{:S(2)}, u32[]{:S(2)}) %all-to-all-start) | async-done | bytes 1048608 | tf_op jit(solution)/shard_map/all_to_all | solution.py:9
  64.7 0.6 fusion.2
  65.3 1.5 %fusion.1 = f32[4096,128]{1,0:T(8,128)} fusion(f32[256,16,128]{2,0,1:T(8,128)S(1)} %get-tuple-element.5, f32[128]{0:T(128)S(1)} %get-tuple-element.4), kind=kLoop, calls=%fused_computation.3 | loop fusion | flops 1048576 | bytes 4194816 | tf_op jit(solution)/shard_map/mul | solution.py:15
Async XLA Ops:
  0.6 1.2 %copy-start = (bf16[256,2048]{1,0:T(8,128)(2,1)S(1)}, bf16[256,2048]{1,0:T(8,128)(2,1)}, u32[]{:S(2)}) copy-start(bf16[256,2048]{1,0:T(8,128)(2,1)} %param.3) | copy-start | bytes 3145732
  1.9 8.5 %copy-start.1 = (bf16[256,2048]{1,0:T(8,128)(2,1)S(1)}, bf16[256,2048]{1,0:T(8,128)(2,1)}, u32[]{:S(2)}) copy-start(bf16[256,2048]{1,0:T(8,128)(2,1)} %param.2) | copy-start | bytes 3145732
  3.1 32.8 %all-to-all-start.1 = ((bf16[256,16,128]{2,0,1:T(8,128)(2,1)}), bf16[256,16,128]{2,0,1:T(8,128)(2,1)S(1)}, u32[]{:S(2)}, u32[]{:S(2)}) async-start(bf16[256,16,128]{2,0,1:T(8,128)(2,1)} %copy_bitcast_fusion), calls=%async_computation.1 | async-start | bytes 2097152 | tf_op jit(solution)/shard_map/all_to_all | solution.py:10
  35.9 28.9 %all-to-all-start = ((bf16[256,16,128]{2,0,1:T(8,128)(2,1)}), bf16[256,16,128]{2,0,1:T(8,128)(2,1)S(1)}, u32[]{:S(2)}, u32[]{:S(2)}) async-start(bf16[256,16,128]{2,0,1:T(8,128)(2,1)} %copy_bitcast_fusion.1), calls=%async_computation | async-start | bytes 2097152 | tf_op jit(solution)/shard_map/all_to_all | solution.py:9
where the time goes:
time: 67.1 us; the launch traced here: 66.8 us
  waiting for transfers between devices  46.4 us (69%)
  starting transfers between devices  12 us (18%)
  other arithmetic  4.06 us (6%)
  local copies, waits for them, and re-layouts  3.71 us (6%)
    all_to_all x1, waiting for transfers between devices, per_device(): lax.all_to_all(second_samples_in, 'dp', split_axis=1, concat_axis=0, tile...  24.3 us
    all_to_all x1, waiting for transfers between devices, per_device(): lax.all_to_all(samples_in, 'dp', split_axis=1, concat_axis=0, tiled=True)  22.1 us
    all_to_all x1, starting transfers between devices, per_device(): lax.all_to_all(second_samples_in, 'dp', split_axis=1, concat_axis=0, tile...  7.22 us
    all_to_all x1, starting transfers between devices, per_device(): lax.all_to_all(samples_in, 'dp', split_axis=1, concat_axis=0, tiled=True)  4.73 us
    mul x1, other arithmetic, per_device(): scaled = power_scaled / sum_scaled * moved_samples_in.shape[0]  1.47 us
    mul x1, other arithmetic, per_device(): power_second_scaled / sum_second_scaled * moved_second_samples_in.shape[0]  1.47 us
  transfers between devices with their start and end apart: 2, of which 2 were waited for; matrix products, arithmetic and copies ran while one was open for 5% of the time, Pallas kernels for 0%

commit v1 on v0

--- a/solution.py
+++ b/solution.py
@@ -4,10 +4,17 @@
 from jax.sharding import PartitionSpec as P
 
 
+def exchange_blocks(block, axis, split, join):
+    size = lax.axis_size(axis)
+    parts = jnp.stack(jnp.split(block, size, axis=split), axis=0)
+    parts = lax.all_to_all(parts, axis, split_axis=0, concat_axis=0)
+    return jnp.concatenate(parts, axis=join)
+
+
 def per_device(samples_in, second_samples_in):
     moved_samples_in, moved_second_samples_in = (
         lax.all_to_all(samples_in, "dp", split_axis=1, concat_axis=0, tiled=True),
-        lax.all_to_all(second_samples_in, "dp", split_axis=1, concat_axis=0, tiled=True),
+        exchange_blocks(second_samples_in, "dp", 1, 0),
     )
     wide_scaled = moved_samples_in.astype(jnp.float32)
     power_scaled = jnp.exp(wide_scaled)

time: 67.1 us -> 88.9 us (1.32)
  local copies, waits for them, and re-layouts: 3.71 us -> 24.9 us
    unnamed x4 -> x17, local copies, waits for them, and re-layouts: 1.23 us -> 22.2 us
    another operation x0 -> x1, local copies, waits for them, and re-layouts: none -> 1.47 us  [exchange_blocks(): parts = jnp.stack(jnp.split(block, size, axis=split), axis=0)]
    all_to_all x1 -> x0, local copies, waits for them, and re-layouts: 1.24 us -> none  [per_device(): lax.all_to_all(second_samples_in, 'dp', split_axis=1, concat_axis=0, tile...]
  transfers between devices with their start and end apart: 2 -> 2, of which waited for: 2 -> 2; matrix products, arithmetic and copies ran while one was open for 5% -> 4% of each run, Pallas kernels for 0% -> 0%
where the time goes in v1:
time: 88.9 us; the launch traced here: 88 us
  waiting for transfers between devices  46.4 us (52%)
  local copies, waits for them, and re-layouts  24.9 us (28%)
  starting transfers between devices  12 us (13%)
  other arithmetic  4.06 us (5%)
    all_to_all x1, waiting for transfers between devices, exchange_blocks(): parts = lax.all_to_all(parts, axis, split_axis=0, concat_axis=0)  24.3 us
    unnamed x17, local copies, waits for them, and re-layouts  22.2 us
    all_to_all x1, waiting for transfers between devices, per_device(): lax.all_to_all(samples_in, 'dp', split_axis=1, concat_axis=0, tiled=True)  22.1 us
    all_to_all x1, starting transfers between devices, exchange_blocks(): parts = lax.all_to_all(parts, axis, split_axis=0, concat_axis=0)  7.22 us
    all_to_all x1, starting transfers between devices, per_device(): lax.all_to_all(samples_in, 'dp', split_axis=1, concat_axis=0, tiled=True)  4.73 us
  transfers between devices with their start and end apart: 2, of which 2 were waited for; matrix products, arithmetic and copies ran while one was open for 4% of the time, Pallas kernels for 0%

profile of v1, /device:TPU:8, one launch (start us, length us, event | category | flops | bytes accessed | tf_op | source)
XLA Modules:
  0.0 88.0 jit_solution(858223437862864179)
XLA Ops:
  0.6 0.0 copy-start
  0.6 1.6 %bitcast_dynamic-update-slice_fusion.15 = bf16[16,256,128]{2,1,0:T(8,128)(2,1)} fusion(bf16[256,2048]{1,0:T(8,128)(2,1)} %param.3), kind=kLoop, calls=%fused_computation.24 | loop fusion | bytes 131072
  2.2 1.5 %bitcast_dynamic-update-slice_fusion.14 = bf16[16,256,128]{2,1,0:T(8,128)(2,1)} fusion(bf16[16,256,128]{2,1,0:T(8,128)(2,1)} %bitcast_dynamic-update-slice_fusion.15, bf16[256,2048]{1,0:T(8,128)(2,1)} %param.3), kind=kLoop, calls=%fused_computation.23 | loop fusion | bytes 131072
  3.7 1.5 %bitcast_dynamic-update-slice_fusion.13 = bf16[16,256,128]{2,1,0:T(8,128)(2,1)} fusion(bf16[16,256,128]{2,1,0:T(8,128)(2,1)} %bitcast_dynamic-update-slice_fusion.14, bf16[256,2048]{1,0:T(8,128)(2,1)} %param.3), kind=kLoop, calls=%fused_computation.22 | loop fusion | bytes 131072
  5.2 1.5 %bitcast_dynamic-update-slice_fusion.12 = bf16[16,256,128]{2,1,0:T(8,128)(2,1)} fusion(bf16[16,256,128]{2,1,0:T(8,128)(2,1)} %bitcast_dynamic-update-slice_fusion.13, bf16[256,2048]{1,0:T(8,128)(2,1)} %param.3), kind=kLoop, calls=%fused_computation.21 | loop fusion | bytes 131072
  6.6 1.5 %bitcast_dynamic-update-slice_fusion.11 = bf16[16,256,128]{2,1,0:T(8,128)(2,1)} fusion(bf16[16,256,128]{2,1,0:T(8,128)(2,1)} %bitcast_dynamic-update-slice_fusion.12, bf16[256,2048]{1,0:T(8,128)(2,1)} %param.3), kind=kLoop, calls=%fused_computation.20 | loop fusion | bytes 131072
  8.1 1.5 %bitcast_dynamic-update-slice_fusion.10 = bf16[16,256,128]{2,1,0:T(8,128)(2,1)} fusion(bf16[16,256,128]{2,1,0:T(8,128)(2,1)} %bitcast_dynamic-update-slice_fusion.11, bf16[256,2048]{1,0:T(8,128)(2,1)} %param.3), kind=kLoop, calls=%fused_computation.19 | loop fusion | bytes 131072
  9.6 1.5 %bitcast_dynamic-update-slice_fusion.9 = bf16[16,256,128]{2,1,0:T(8,128)(2,1)} fusion(bf16[16,256,128]{2,1,0:T(8,128)(2,1)} %bitcast_dynamic-update-slice_fusion.10, bf16[256,2048]{1,0:T(8,128)(2,1)} %param.3), kind=kLoop, calls=%fused_computation.18 | loop fusion | bytes 131072
  11.0 1.5 %bitcast_dynamic-update-slice_fusion.8 = bf16[16,256,128]{2,1,0:T(8,128)(2,1)} fusion(bf16[16,256,128]{2,1,0:T(8,128)(2,1)} %bitcast_dynamic-update-slice_fusion.9, bf16[256,2048]{1,0:T(8,128)(2,1)} %param.3), kind=kLoop, calls=%fused_computation.17 | loop fusion | bytes 131072
  12.5 1.5 %bitcast_dynamic-update-slice_fusion.7 = bf16[16,256,128]{2,1,0:T(8,128)(2,1)} fusion(bf16[16,256,128]{2,1,0:T(8,128)(2,1)} %bitcast_dynamic-update-slice_fusion.8, bf16[256,2048]{1,0:T(8,128)(2,1)} %param.3), kind=kLoop, calls=%fused_computation.16 | loop fusion | bytes 131072
  14.0 1.5 %bitcast_dynamic-update-slice_fusion.6 = bf16[16,256,128]{2,1,0:T(8,128)(2,1)} fusion(bf16[16,256,128]{2,1,0:T(8,128)(2,1)} %bitcast_dynamic-update-slice_fusion.7, bf16[256,2048]{1,0:T(8,128)(2,1)} %param.3), kind=kLoop, calls=%fused_computation.15 | loop fusion | bytes 131072
  15.5 1.5 %bitcast_dynamic-update-slice_fusion.5 = bf16[16,256,128]{2,1,0:T(8,128)(2,1)} fusion(bf16[16,256,128]{2,1,0:T(8,128)(2,1)} %bitcast_dynamic-update-slice_fusion.6, bf16[256,2048]{1,0:T(8,128)(2,1)} %param.3), kind=kLoop, calls=%fused_computation.14 | loop fusion | bytes 131072
  16.9 1.5 %bitcast_dynamic-update-slice_fusion.4 = bf16[16,256,128]{2,1,0:T(8,128)(2,1)} fusion(bf16[16,256,128]{2,1,0:T(8,128)(2,1)} %bitcast_dynamic-update-slice_fusion.5, bf16[256,2048]{1,0:T(8,128)(2,1)} %param.3), kind=kLoop, calls=%fused_computation.13 | loop fusion | bytes 131072
  18.4 1.5 %bitcast_dynamic-update-slice_fusion.3 = bf16[16,256,128]{2,1,0:T(8,128)(2,1)} fusion(bf16[16,256,128]{2,1,0:T(8,128)(2,1)} %bitcast_dynamic-update-slice_fusion.4, bf16[256,2048]{1,0:T(8,128)(2,1)} %param.3), kind=kLoop, calls=%fused_computation.12 | loop fusion | bytes 131072
  19.9 1.5 %bitcast_dynamic-update-slice_fusion.2 = bf16[16,256,128]{2,1,0:T(8,128)(2,1)} fusion(bf16[16,256,128]{2,1,0:T(8,128)(2,1)} %bitcast_dynamic-update-slice_fusion.3, bf16[256,2048]{1,0:T(8,128)(2,1)} %param.3), kind=kLoop, calls=%fused_computation.11 | loop fusion | bytes 131072
  21.4 1.5 %bitcast_dynamic-update-slice_fusion.1 = bf16[16,256,128]{2,1,0:T(8,128)(2,1)} fusion(bf16[16,256,128]{2,1,0:T(8,128)(2,1)} %bitcast_dynamic-update-slice_fusion.2, bf16[256,2048]{1,0:T(8,128)(2,1)} %param.3), kind=kLoop, calls=%fused_computation.10 | loop fusion | bytes 131072
  22.8 1.5 %bitcast_dynamic-update-slice_fusion = bf16[16,256,128]{2,1,0:T(8,128)(2,1)} fusion(bf16[16,256,128]{2,1,0:T(8,128)(2,1)} %bitcast_dynamic-update-slice_fusion.1, bf16[256,2048]{1,0:T(8,128)(2,1)} %param.3), kind=kLoop, calls=%fused_computation.9 | loop fusion | bytes 131072 | tf_op jit(solution)/shard_map/stack | solution.py:9
  24.3 7.2 %all-to-all-start.1 = ((bf16[16,256,128]{2,1,0:T(8,128)(2,1)}), bf16[16,256,128]{2,1,0:T(8,128)(2,1)S(1)}, u32[]{:S(2)}, u32[]{:S(2)}) async-start(bf16[16,256,128]{2,1,0:T(8,128)(2,1)} %bitcast_dynamic-update-slice_fusion), calls=%async_computation.1 | async-start | bytes 2097152 | tf_op jit(solution)/shard_map/all_to_all | solution.py:10
  31.5 0.0 copy-done
  31.5 1.2 %copy_bitcast_fusion = bf16[256,16,128]{2,0,1:T(8,128)(2,1)} fusion(bf16[256,2048]{1,0:T(8,128)(2,1)S(1)} %copy-done), kind=kLoop, calls=%fused_computation.6 | loop fusion | bytes 2097152 | tf_op jit(solution)/shard_map/all_to_all | solution.py:16
  32.8 24.3 %all-to-all-done.1 = bf16[16,256,128]{2,1,0:T(8,128)(2,1)S(1)} async-done(((bf16[16,256,128]{2,1,0:T(8,128)(2,1)}), bf16[16,256,128]{2,1,0:T(8,128)(2,1)S(1)}, u32[]{:S(2)}, u32[]{:S(2)}) %all-to-all-start.1) | async-done | bytes 1048608 | tf_op jit(solution)/shard_map/all_to_all | solution.py:10
  57.1 4.7 %all-to-all-start = ((bf16[256,16,128]{2,0,1:T(8,128)(2,1)}), bf16[256,16,128]{2,0,1:T(8,128)(2,1)S(1)}, u32[]{:S(2)}, u32[]{:S(2)}) async-start(bf16[256,16,128]{2,0,1:T(8,128)(2,1)} %copy_bitcast_fusion), calls=%async_computation | async-start | bytes 2097152 | tf_op jit(solution)/shard_map/all_to_all | solution.py:16
  61.8 0.6 fusion.3
  62.4 1.5 %fusion.1 = f32[4096,128]{1,0:T(8,128)} fusion(f32[16,256,128]{2,1,0:T(8,128)S(1)} %get-tuple-element.3, f32[128]{0:T(128)S(1)} %get-tuple-element.2), kind=kLoop, calls=%fused_computation.3 | loop fusion | flops 1048576 | bytes 4194816 | tf_op jit(solution)/shard_map/mul | solution.py:26
  63.8 22.1 %all-to-all-done = bf16[256,16,128]{2,0,1:T(8,128)(2,1)S(1)} async-done(((bf16[256,16,128]{2,0,1:T(8,128)(2,1)}), bf16[256,16,128]{2,0,1:T(8,128)(2,1)S(1)}, u32[]{:S(2)}, u32[]{:S(2)}) %all-to-all-start) | async-done | bytes 1048608 | tf_op jit(solution)/shard_map/all_to_all | solution.py:16
  85.9 0.6 fusion.2
  86.5 1.5 %fusion = f32[4096,128]{1,0:T(8,128)} fusion(f32[256,16,128]{2,0,1:T(8,128)S(1)} %get-tuple-element.5, f32[128]{0:T(128)S(1)} %get-tuple-element.4), kind=kLoop, calls=%fused_computation.1 | loop fusion | flops 1048576 | bytes 4194816 | tf_op jit(solution)/shard_map/mul | solution.py:22
Async XLA Ops:
  0.6 30.9 %copy-start = (bf16[256,2048]{1,0:T(8,128)(2,1)S(1)}, bf16[256,2048]{1,0:T(8,128)(2,1)}, u32[]{:S(2)}) copy-start(bf16[256,2048]{1,0:T(8,128)(2,1)} %param.2) | copy-start | bytes 3145732
  24.3 32.8 %all-to-all-start.1 = ((bf16[16,256,128]{2,1,0:T(8,128)(2,1)}), bf16[16,256,128]{2,1,0:T(8,128)(2,1)S(1)}, u32[]{:S(2)}, u32[]{:S(2)}) async-start(bf16[16,256,128]{2,1,0:T(8,128)(2,1)} %bitcast_dynamic-update-slice_fusion), calls=%async_computation.1 | async-start | bytes 2097152 | tf_op jit(solution)/shard_map/all_to_all | solution.py:10
  57.1 28.9 %all-to-all-start = ((bf16[256,16,128]{2,0,1:T(8,128)(2,1)}), bf16[256,16,128]{2,0,1:T(8,128)(2,1)S(1)}, u32[]{:S(2)}, u32[]{:S(2)}) async-start(bf16[256,16,128]{2,0,1:T(8,128)(2,1)} %copy_bitcast_fusion), calls=%async_computation | async-start | bytes 2097152 | tf_op jit(solution)/shard_map/all_to_all | solution.py:16
